TPU v7x, 256 devices: a whole 4x4x8 slice. The times are simulated.
256 devices in a mesh: cuts: 16 (over z_lo, y, core), sub: 16 (over z_hi, x).
Axes of the slice: x: 4, y: 4, z: 8 (z_hi: 4, z_lo: 2; z = z_hi * 2 + z_lo), core: 2. Of those that a mesh axis runs over, the one named last changes fastest.
Arguments:
- start_states: float32 [16, 32, 512, 128], P('cuts', 'sub'), may hold values from -8 to 8
- source: bfloat16 [32, 512, 128], P('sub'), may hold values from -3 to 3
- block_inverse: bfloat16 [32, 512, 512], P('sub'), may hold values from -1 to 1
- face_map: int32 [32, 2, 128], P('sub'), may hold values from 0 to 127, each once within a row
- transmissibility: float32 [32, 2, 128], P('sub'), may hold values from 7 to 11
- partner: int32 [32], replicated, may hold values from 0 to 31
- fracture_cond: float32 [32], replicated, may hold values from 0.3 to 3
Outputs:
- new_starts: float32 [16, 32, 512, 128], P('cuts', 'sub')
All inputs are finite; a program needn't handle non-finite values.
Results may differ from a plain program's by a relative error of at most 0.0024.
Values sent between devices are 32-bit elements; how exact they have to be, the bound alone decides.
A program may use at most 64 MiB of HBM per device.

v0:
```python
import functools

import jax
import jax.numpy as jnp
from jax import lax
from jax.experimental import pallas as pl
from jax.experimental.pallas import tpu as pltpu
from jax.sharding import PartitionSpec as P

F = 128
STEPS = 4
MESH = pl.DeviceIdType.MESH
f32, bf16 = jnp.float32, jnp.bfloat16
HI = lax.Precision.HIGHEST
PF, Q1, U2, Q3, MM, SR, MT = range(7)


def dot(a, b):
    return jnp.dot(a, b, preferred_element_type=f32)


def chosen(row):
    places = lax.broadcasted_iota(jnp.int32, (F, F), 0).astype(f32)
    hot = jnp.where(places == jnp.broadcast_to(row, (F, F)), 1.0, 0.0).astype(f32)
    return hot.T.astype(bf16)


def down_rows(row):
    return jnp.broadcast_to(row, (F, F)).T


def pick(hot, x):
    high = x.astype(bf16)
    low = (x - high.astype(f32)).astype(bf16)
    both = dot(hot, jnp.concatenate([high, low], axis=1))
    return both[:, :F] + both[:, F:]


def kernel(ns, nc, partner, cond, start_h, source_h, inv_h, fmap, trans, out,
           state, src, inv, rhs, v, sbuf, rbuf, smt, rmt, inn, gin, rg, tb, tg, hot, ghot,
           bp, xp, mp, prev, scoarse, rcoarse, hs, zb, zs, hb, gm, rm,
           lsem, ssem, rsem, esem, resem, csem, rcsem, hsem, rhsem, zsem, rzsem):
    c, s = lax.axis_index("cuts"), lax.axis_index("sub")
    width = state.shape[1]
    lo, hi = slice(0, F), slice(width - F, width)
    has_below, has_above = s > 0, s < ns - 1

    loads = [
        pltpu.make_async_copy(start_h.at[0], state, lsem.at[0]),
        pltpu.make_async_copy(source_h, src, lsem.at[1]),
        pltpu.make_async_copy(inv_h, inv, lsem.at[2]),
    ]
    for load in loads:
        load.start()

    hs[...] = jnp.zeros_like(hs)
    hb[...] = jnp.zeros_like(hb)
    rcoarse[...] = jnp.zeros_like(rcoarse)

    barrier = pltpu.get_barrier_semaphore()
    for o in range(1, ns):
        pl.semaphore_signal(barrier, inc=1, device_id={"sub": lax.rem(s + o, ns)}, device_id_type=MESH)
    for o in range(1, nc):
        pl.semaphore_signal(barrier, inc=1, device_id={"cuts": lax.rem(c + o, nc)}, device_id_type=MESH)

    def ext(d, i):
        to = lax.rem(s + 1, ns) if d == 0 else lax.rem(s + ns - 1, ns)
        if i == MT:
            a, b = smt.at[d], rmt.at[d]
        elif i == PF:
            a = state.at[1, pl.ds(width - F, F)] if d == 0 else state.at[0, pl.ds(0, F)]
            b = rbuf.at[d, i]
        else:
            a, b = sbuf.at[d, i], rbuf.at[d, i]
        return pltpu.make_async_remote_copy(
            src_ref=a, dst_ref=b, send_sem=ssem.at[d, i], recv_sem=rsem.at[d, i],
            device_id={"sub": to}, device_id_type=MESH)

    sends = (has_above, has_below)
    recvs = (has_below, has_above)

    def send(d, *which):
        @pl.when(sends[d])
        def _():
            for i in which:
                ext(d, i).start()

    def sent(*which):
        for d in (0, 1):
            @pl.when(sends[d])
            def _():
                for i in which:
                    ext(d, i).wait_send()

    def arrive(*which):
        for d in (0, 1):
            @pl.when(recvs[d])
            def _():
                for i in which:
                    ext(d, i).wait_recv()

    for d in (0, 1):
        @pl.when(jnp.logical_not(recvs[d]))
        def _():
            rbuf[d] = jnp.zeros(rbuf.shape[1:], f32)
            rmt[d] = jnp.zeros(rmt.shape[1:], f32)

    rows = [[fmap[b, pl.ds(k, 1), :].astype(f32) for k in (0, 1)] for b in (0, 1)]
    trow = [[trans[b, pl.ds(k, 1), :] for k in (0, 1)] for b in (0, 1)]
    for b in (0, 1):
        for k in (0, 1):
            tb[b, k] = down_rows(trow[b][k])
            hot[b, k] = chosen(rows[b][k])
    smt[...] = jnp.zeros_like(smt)
    smt[0, pl.ds(0, 1), :] = rows[1][1]
    smt[0, pl.ds(1, 1), :] = trow[1][1]
    smt[1, pl.ds(0, 1), :] = rows[0][0]
    smt[1, pl.ds(1, 1), :] = trow[0][0]

    loads[0].wait()
    @pl.when(c == 0)
    def _():
        prev[...] = state[...]
    scoarse[...] = jnp.zeros_like(scoarse)
    for b in (0, 1):
        scoarse[pl.ds(b, 1), :] = jnp.sum(state[b], axis=0, keepdims=True) / width

    pl.semaphore_wait(barrier, ns - 1 + nc - 1)

    for d in (0, 1):
        send(d, PF, MT)

    def coarse_back():
        return pltpu.make_async_remote_copy(
            src_ref=scoarse, dst_ref=rcoarse, send_sem=csem, recv_sem=rcsem,
            device_id={"cuts": lax.rem(c + nc - 1, nc)}, device_id_type=MESH)

    @pl.when(c > 0)
    def _():
        coarse_back().start()

    loads[1].wait()
    loads[2].wait()
    sbuf[0, MM] = inv[1, hi, hi].astype(f32)
    sbuf[1, MM] = inv[0, lo, lo].astype(f32)
    sbuf[0, SR] = src[1, hi].astype(f32)
    sbuf[1, SR] = src[0, lo].astype(f32)
    for d in (0, 1):
        send(d, MM, SR)

    bp[0] = dot(hot[1, 0], inv[0, hi, :]).astype(bf16)
    bp[1] = dot(hot[0, 1], inv[1, lo, :]).astype(bf16)
    inn[0] = pick(hot[1, 0], state[0, hi])
    inn[1] = pick(hot[0, 1], state[1, lo])

    def inner_faces():
        v[0, hi] = (rhs[0, hi] + tb[0, 1] * inn[1]).astype(bf16)
        v[1, lo] = (rhs[1, lo] + tb[1, 0] * inn[0]).astype(bf16)

    def inner_sweep():
        inn[0] = dot(bp[0], v[0])
        inn[1] = dot(bp[1], v[1])

    def outer_faces(below, above):
        v[0, lo] = (rhs[0, lo] + tb[0, 0] * below).astype(bf16)
        v[1, hi] = (rhs[1, hi] + tb[1, 1] * above).astype(bf16)

    def ghost(d):
        return dot(mp[d], (rg[d] + tg[d] * gin[d]).astype(bf16))

    npad = gm.shape[0]
    ri = lax.broadcasted_iota(jnp.int32, (npad, npad), 0)
    ci = lax.broadcasted_iota(jnp.int32, (npad, npad), 1)

    def coarse_inverse():
        def place(b):
            return 8 * lax.shift_right_logical(b, 1) + lax.bitwise_and(b, 1)

        def link(b, w):
            q = partner[b]
            at, to, g = place(b), place(q), cond[b]
            w = w + jnp.where((ri == at) & (ci == to), g, 0.0)
            return w + jnp.where((ri == to) & (ci == at), g, 0.0)

        real_r = lax.bitwise_and(ri, 7) < 2
        real_c = lax.bitwise_and(ci, 7) < 2
        br, bc = place_back(ri), place_back(ci)
        chain = jnp.where(real_r & real_c & ((br - bc == 1) | (bc - br == 1)), 1.0, 0.0).astype(f32)
        w = lax.fori_loop(0, 2 * ns, link, chain)
        total = jnp.sum(w, axis=1, keepdims=True)
        system = jnp.where(ri == ci, 1.0 + total, 0.0) - w

        def pivot(b, a):
            at = place(b)
            col = jnp.sum(jnp.where(ci == at, a, 0.0), axis=1, keepdims=True)
            row = jnp.sum(jnp.where(ri == at, a, 0.0), axis=0, keepdims=True)
            d = jnp.sum(jnp.where((ci == at) & (ri == at), a, 0.0), axis=(0, 1), keepdims=True)
            inv_d = 1.0 / d
            new = a - col * (row * inv_d)
            new = jnp.where(ri == at, row * inv_d, new)
            new = jnp.where(ci == at, col * inv_d, new)
            return jnp.where((ci == at) & (ri == at), -inv_d, new)

        gm[...] = -lax.fori_loop(0, 2 * ns, pivot, system)
        rm[...] = jnp.zeros_like(rm)

    def place_back(i):
        return 2 * lax.shift_right_logical(i, 3) + lax.bitwise_and(i, 7)

    rr = lax.broadcasted_iota(jnp.int32, rm.shape, 0)
    rc = lax.broadcasted_iota(jnp.int32, rm.shape, 1)

    def coarse_powers(first, count):
        def one(i, _):
            k = nc - 1 - first - i
            j = c - 1 - k
            unit = lax.bitwise_and(rr, 7)
            same = (unit < 2) & (unit == lax.bitwise_and(rc, 7))
            here = same & (rr - unit == 8 * s) & (rc - unit == 8 * j) & (k >= 1)
            rm[...] = jnp.dot(gm[...], rm[...] + jnp.where(here, 1.0, 0.0), precision=HI,
                              preferred_element_type=f32)
            return 0
        lax.fori_loop(0, count, one, 0)

    half = nc // 2

    def step(n, _):
        for b in (0, 1):
            r = state[b] + src[b].astype(f32)
            rhs[b] = r
            v[b] = r.astype(bf16)
        inner_faces()
        sbuf[0, Q1] = dot(inv[1, hi, 0:width - F], v[1, 0:width - F])
        send(0, Q1)
        sbuf[1, Q1] = dot(inv[0, lo, F:width], v[0, F:width])
        send(1, Q1)

        @pl.when(n == 1)
        def _():
            coarse_inverse()

        @pl.when(n == 2)
        def _():
            coarse_powers(half, nc - 1 - half)

        @pl.when(n == 0)
        def _():
            arrive(MT)
            for d in (0, 1):
                ghot[d] = chosen(rmt[d, pl.ds(0, 1), :])
                tg[d] = down_rows(rmt[d, pl.ds(1, 1), :])
            xp[0] = dot(ghot[0], inv[0, lo, :]).astype(bf16)
            xp[1] = dot(ghot[1], inv[1, hi, :]).astype(bf16)
            gin[0] = pick(ghot[0], state[0, lo])
            gin[1] = pick(ghot[1], state[1, hi])

        arrive(PF)
        outer_faces(pick(hot[0, 0], rbuf[0, PF]), pick(hot[1, 1], rbuf[1, PF]))
        inner_sweep()

        @pl.when(n == 0)
        def _():
            arrive(MM, SR)
            mp[0] = dot(hot[0, 0], rbuf[0, MM].astype(bf16)).astype(bf16)
            mp[1] = dot(hot[1, 1], rbuf[1, MM].astype(bf16)).astype(bf16)
            sent(MM, SR, MT)

        for d in (0, 1):
            rg[d] = rbuf[d, PF] + rbuf[d, SR]
        own = [ghost(d) for d in (0, 1)]
        arrive(Q1)
        below = pick(hot[0, 0], rbuf[0, Q1]) + own[0]
        above = pick(hot[1, 1], rbuf[1, Q1]) + own[1]
        sent(PF, Q1)

        outer_faces(below, above)
        inner_faces()
        up = dot(xp[1], v[1])
        sbuf[0, U2] = up
        gin[1] = up
        send(0, U2)
        down = dot(xp[0], v[0])
        sbuf[1, U2] = down
        gin[0] = down
        send(1, U2)
        inner_sweep()
        inner_faces()
        sbuf[0, Q3] = dot(xp[1, :, 0:width - F], v[1, 0:width - F])
        send(0, Q3)
        sbuf[1, Q3] = dot(xp[0, :, F:width], v[0, F:width])
        send(1, Q3)

        @pl.when(n == 1)
        def _():
            coarse_powers(0, half)

        own = [ghost(d) for d in (0, 1)]
        arrive(U2)
        outer_faces(rbuf[0, U2], rbuf[1, U2])
        inner_sweep()
        arrive(Q3)
        below = rbuf[0, Q3] + own[0]
        above = rbuf[1, Q3] + own[1]
        sent(U2, Q3)

        outer_faces(below, above)
        inner_faces()
        state[1, hi] = dot(inv[1, hi, :], v[1])
        state[0, lo] = dot(inv[0, lo, :], v[0])

        @pl.when(n < STEPS - 1)
        def _():
            send(0, PF)
            send(1, PF)

        state[0, F:width] = dot(inv[0, F:width, :], v[0])
        state[1, 0:width - F] = dot(inv[1, 0:width - F, :], v[1])

        @pl.when(n < STEPS - 1)
        def _():
            inner_sweep()
            gin[0] = dot(xp[0], v[0])
            gin[1] = dot(xp[1], v[1])
        return 0

    lax.fori_loop(0, STEPS, step, 0)

    def end(b):
        return pltpu.make_async_remote_copy(
            src_ref=state.at[b], dst_ref=prev.at[b], send_sem=esem.at[b], recv_sem=resem.at[b],
            device_id={"cuts": lax.rem(c + 1, nc)}, device_id_type=MESH)

    def jump(o):
        return pltpu.make_async_remote_copy(
            src_ref=hb, dst_ref=hs.at[c], send_sem=hsem.at[o], recv_sem=rhsem.at[c],
            device_id={"cuts": lax.rem(c + o, nc)}, device_id_type=MESH)

    def jump_from(o):
        at = lax.rem(c + nc - o, nc)
        return pltpu.make_async_remote_copy(
            src_ref=hb, dst_ref=hs.at[at], send_sem=hsem.at[o], recv_sem=rhsem.at[at],
            device_id={"cuts": at}, device_id_type=MESH)

    def part(o):
        to = lax.rem(s + o, ns)
        return pltpu.make_async_remote_copy(
            src_ref=zb.at[to], dst_ref=zs.at[s], send_sem=zsem.at[o], recv_sem=rzsem.at[s],
            device_id={"sub": to}, device_id_type=MESH)

    def part_from(o):
        at = lax.rem(s + ns - o, ns)
        return pltpu.make_async_remote_copy(
            src_ref=zb.at[at], dst_ref=zs.at[at], send_sem=zsem.at[o], recv_sem=rzsem.at[at],
            device_id={"sub": at}, device_id_type=MESH)

    @pl.when(c < nc - 1)
    def _():
        coarse_back().wait_recv()

    for b in (0, 1):
        hb[pl.ds(b, 1), :] = jnp.sum(state[b], axis=0, keepdims=True) / width - rcoarse[pl.ds(b, 1), :]
    for o in range(2, nc):
        @pl.when(c + o < nc)
        def _():
            jump(o).start()

    @pl.when(c < nc - 1)
    def _():
        for b in (0, 1):
            end(b).start()

    @pl.when(c > 0)
    def _():
        coarse_back().wait_send()

    for o in range(2, nc):
        @pl.when(c - o >= 0)
        def _():
            jump_from(o).wait_recv()

    z = jnp.dot(rm[...], hs[...].reshape(8 * nc, F), precision=HI, preferred_element_type=f32)
    zb[...] = z.reshape(ns, 8, F)
    for o in range(1, ns):
        part(o).start()
    for o in range(1, ns):
        part_from(o).wait_recv()
    zs[s] = zb[s]
    w = jnp.sum(zs[...], axis=0)

    @pl.when(c > 0)
    def _():
        for b in (0, 1):
            end(b).wait_recv()

    for b in (0, 1):
        out[0, b] = prev[b] + jnp.broadcast_to(w[b:b + 1], (width, F))

    for o in range(2, nc):
        @pl.when(c + o < nc)
        def _():
            jump(o).wait_send()
    for o in range(1, ns):
        part(o).wait_send()

    @pl.when(c < nc - 1)
    def _():
        for b in (0, 1):
            end(b).wait_send()


def solution(mesh):
    ns, nc = mesh.shape["sub"], mesh.shape["cuts"]

    def on_device(start, source, inverse, face_map, trans, partner, cond):
        width, cols = start.shape[2:]
        any_ = pl.BlockSpec(memory_space=pl.ANY)
        vmem = pl.BlockSpec(memory_space=pltpu.VMEM)
        smem = pl.BlockSpec(memory_space=pltpu.SMEM)
        V, S = pltpu.VMEM, pltpu.SemaphoreType.DMA
        scratch = dict(
            state=V((2, width, cols), f32), src=V((2, width, cols), bf16), inv=V((2, width, width), bf16),
            rhs=V((2, width, cols), f32), v=V((2, width, cols), bf16),
            sbuf=V((2, 6, F, cols), f32), rbuf=V((2, 6, F, cols), f32),
            smt=V((2, 8, F), f32), rmt=V((2, 8, F), f32),
            inn=V((2, F, cols), f32), gin=V((2, F, cols), f32), rg=V((2, F, cols), f32),
            tb=V((2, 2, F, cols), f32), tg=V((2, F, cols), f32),
            hot=V((2, 2, F, F), bf16), ghot=V((2, F, F), bf16),
            bp=V((2, F, width), bf16), xp=V((2, F, width), bf16), mp=V((2, F, F), bf16),
            prev=V((2, width, cols), f32), scoarse=V((8, cols), f32), rcoarse=V((8, cols), f32),
            hs=V((nc, 8, cols), f32), zb=V((ns, 8, cols), f32), zs=V((ns, 8, cols), f32),
            hb=V((8, cols), f32), gm=V((8 * ns, 8 * ns), f32), rm=V((8 * ns, 8 * nc), f32),
            lsem=S((3,)), ssem=S((2, 7)), rsem=S((2, 7)), esem=S((2,)), resem=S((2,)),
            csem=S(()), rcsem=S(()), hsem=S((nc,)), rhsem=S((nc,)), zsem=S((ns,)), rzsem=S((ns,)),
        )
        return pl.pallas_call(
            functools.partial(kernel, ns, nc),
            out_shape=jax.ShapeDtypeStruct(start.shape, f32),
            in_specs=[smem, smem, any_, any_, any_, vmem, vmem],
            out_specs=vmem,
            scratch_shapes=list(scratch.values()),
            compiler_params=pltpu.CompilerParams(collective_id=0, has_side_effects=True),
            name="parareal",
        )(partner, cond, start, source, inverse, face_map, trans)

    in_specs = (
        P("cuts", "sub", None, None),
        P("sub", None, None),
        P("sub", None, None),
        P("sub", None, None),
        P("sub", None, None),
        P(),
        P(),
    )
    return jax.shard_map(on_device, mesh=mesh, in_specs=in_specs,
                         out_specs=P("cuts", "sub", None, None), check_vma=False)
```

profile of v0, /device:TPU:32, one launch (start us, length us, event | category | flops | bytes accessed | tf_op | source)
XLA Modules:
  0.0 96.9 jit_solution(13631087782790532041)
XLA Ops:
  0.0 95.0 %parareal.1 = f32[1,2,512,128]{3,2,1,0:T(8,128)} custom-call(s32[32]{0:T(128)} %partner.1, f32[32]{0:T(128)} %cond.1, f32[1,2,512,128]{3,2,1,0:T(8,128)} %start_h.1, bf16[2,512,128]{2,1,0:T(8,128)(2,1)} %source_h.1, bf16[2,512,512]{2,1,0:T(8,128)(2,1)} %inv_h.1, s32[2,2,128]{2,1,0:T(2,128)} %fmap.1, f32[2,2,128]{2,1,0:T(2,128)} %trans.1), custom_call_target="tpu_custom_call" | custom-call | tf_op jit(solution)/shard_map/parareal/pallas_call | solution.py:435
  95.0 1.9 %copy.9 = f32[1,2,512,128]{3,2,1,0:T(8,128)} copy(f32[1,2,512,128]{3,2,1,0:T(8,128)} %parareal.1) | data formatting | bytes 1048576
where the time goes:
time: 97.9 us; the launch traced here: 96.9 us
  Pallas kernels  95 us (97%)
  local copies, waits for them, and re-layouts  1.87 us (2%)
    pallas_call x1, Pallas kernels, on_device(): pl.pallas_call(functools.partial(kernel, ns, nc), out_shape=jax.ShapeDtyp...  95 us

commit v1 on v0

v1 whole, which is shorter than its diff:
```python
import functools

import jax
import jax.numpy as jnp
from jax import lax
from jax.experimental import pallas as pl
from jax.experimental.pallas import tpu as pltpu
from jax.sharding import PartitionSpec as P

F = 128
STEPS = 4
MESH = pl.DeviceIdType.MESH
f32, bf16 = jnp.float32, jnp.bfloat16
HI = lax.Precision.HIGHEST
PF, Q1, U2, Q3, MT = range(5)


def dot(a, b):
    return jnp.dot(a, b, preferred_element_type=f32)


def chosen(row):
    places = lax.broadcasted_iota(jnp.int32, (F, F), 0).astype(f32)
    hot = jnp.where(places == jnp.broadcast_to(row, (F, F)), 1.0, 0.0).astype(f32)
    return hot.T.astype(bf16)


def down_rows(row):
    return jnp.broadcast_to(row, (F, F)).T


def pick(hot, x):
    high = x.astype(bf16)
    low = (x - high.astype(f32)).astype(bf16)
    both = dot(hot, jnp.concatenate([high, low], axis=1))
    return both[:, :F] + both[:, F:]


def kernel(ns, nc, partner, cond, start_h, source_h, inv_h, fmap, trans, prev, wout,
           state, src, inv, face, rf, vf, vi, cn, ci, bx, bi, sbuf, rbuf, smt, rmt, sst, rst,
           inn, gin, rg, tb, tg, hot, ghot, mp, scoarse, rcoarse, hs, zb, zs, hb, gm, rm, rw,
           lsem, ssem, rsem, psem, rpsem, fsem, rfsem, esem, resem, csem, rcsem, hsem, rhsem, zsem, rzsem):
    c, s = lax.axis_index("cuts"), lax.axis_index("sub")
    width = state.shape[1]
    L, U, I = slice(0, F), slice(width - F, width), slice(F, width - F)
    fL, fU = slice(0, F), slice(F, 2 * F)
    has_below, has_above = s > 0, s < ns - 1

    loads = [
        pltpu.make_async_copy(start_h.at[0], state, lsem.at[0]),
        pltpu.make_async_copy(source_h, src, lsem.at[1]),
        pltpu.make_async_copy(inv_h, inv, lsem.at[2]),
    ]
    for load in loads:
        load.start()

    hs[...] = jnp.zeros_like(hs)
    hb[...] = jnp.zeros_like(hb)
    rcoarse[...] = jnp.zeros_like(rcoarse)

    barrier = pltpu.get_barrier_semaphore()
    for o in range(1, ns):
        pl.semaphore_signal(barrier, inc=1, device_id={"sub": lax.rem(s + o, ns)}, device_id_type=MESH)
    for o in range(1, nc):
        pl.semaphore_signal(barrier, inc=1, device_id={"cuts": lax.rem(c + o, nc)}, device_id_type=MESH)

    def towards(d):
        return lax.rem(s + 1, ns) if d == 0 else lax.rem(s + ns - 1, ns)

    def ext(d, i):
        if i == MT:
            a, b = smt.at[d], rmt.at[d]
        elif i == PF:
            a = state.at[1, pl.ds(width - F, F)] if d == 0 else state.at[0, pl.ds(0, F)]
            b = rbuf.at[d, i]
        else:
            a, b = sbuf.at[d, i], rbuf.at[d, i]
        return pltpu.make_async_remote_copy(
            src_ref=a, dst_ref=b, send_sem=ssem.at[d, i], recv_sem=rsem.at[d, i],
            device_id={"sub": towards(d)}, device_id_type=MESH)

    sends = (has_above, has_below)
    recvs = (has_below, has_above)

    def send(d, *which):
        @pl.when(sends[d])
        def _():
            for i in which:
                ext(d, i).start()

    def sent(*which):
        for d in (0, 1):
            @pl.when(sends[d])
            def _():
                for i in which:
                    ext(d, i).wait_send()

    def arrive(*which):
        for d in (0, 1):
            @pl.when(recvs[d])
            def _():
                for i in which:
                    ext(d, i).wait_recv()

    group = min(8, nc)
    size = F // group
    own = lax.rem(c, group)

    def piece(ref, d, at):
        return ref.at[d, :, pl.ds(pl.multiple_of(at * size, size), size)]

    def across(d):
        return pltpu.make_async_remote_copy(
            src_ref=piece(sst, d, own), dst_ref=piece(rst, d, own), send_sem=psem.at[d], recv_sem=rpsem.at[d],
            device_id={"sub": towards(d)}, device_id_type=MESH)

    def along(d, o):
        return pltpu.make_async_remote_copy(
            src_ref=piece(rst, d, own), dst_ref=piece(rst, d, own), send_sem=fsem.at[d, o],
            recv_sem=rfsem.at[d, own], device_id={"cuts": c - own + lax.rem(own + o, group)}, device_id_type=MESH)

    def along_from(d, o):
        at = lax.rem(own + group - o, group)
        return pltpu.make_async_remote_copy(
            src_ref=piece(rst, d, at), dst_ref=piece(rst, d, at), send_sem=fsem.at[d, o],
            recv_sem=rfsem.at[d, at], device_id={"cuts": c - own + at}, device_id_type=MESH)

    for d in (0, 1):
        @pl.when(jnp.logical_not(recvs[d]))
        def _():
            rbuf[d] = jnp.zeros(rbuf.shape[1:], f32)
            rmt[d] = jnp.zeros(rmt.shape[1:], f32)
            rst[d] = jnp.zeros(rst.shape[1:], f32)

    rows = [[fmap[b, pl.ds(k, 1), :].astype(f32) for k in (0, 1)] for b in (0, 1)]
    trow = [[trans[b, pl.ds(k, 1), :] for k in (0, 1)] for b in (0, 1)]
    smt[...] = jnp.zeros_like(smt)
    smt[0, pl.ds(0, 1), :] = rows[1][1]
    smt[0, pl.ds(1, 1), :] = trow[1][1]
    smt[1, pl.ds(0, 1), :] = rows[0][0]
    smt[1, pl.ds(1, 1), :] = trow[0][0]
    for b in (0, 1):
        for k in (0, 1):
            tb[b, k] = down_rows(trow[b][k])
            hot[b, k] = chosen(rows[b][k])

    loads[0].wait()
    keep = pltpu.make_async_copy(state, prev, lsem.at[3])

    @pl.when(c == 0)
    def _():
        keep.start()

    loads[1].wait()
    sst[0, 1] = src[1, U].astype(f32)
    sst[1, 1] = src[0, L].astype(f32)
    loads[2].wait()
    sst[0, 0] = inv[1, U, U].astype(f32)
    sst[1, 0] = inv[0, L, L].astype(f32)

    pl.semaphore_wait(barrier, ns - 1 + nc - 1)

    for d in (0, 1):
        send(d, MT, PF)

        @pl.when(sends[d])
        def _():
            across(d).start()

    def own_rows(b):
        rows_of = dot(hot[1, 0], inv[0, U, :]) if b == 0 else dot(hot[0, 1], inv[1, L, :])
        rows_of = rows_of.astype(bf16)
        bx[b, F:, fL] = rows_of[:, L]
        bx[b, F:, fU] = rows_of[:, U]
        bi[b, F:] = rows_of[:, I]

    inn[0] = pick(hot[1, 0], state[0, U])
    inn[1] = pick(hot[0, 1], state[1, L])

    def inner_faces():
        vf[0, fU] = (rf[0, fU] + tb[0, 1] * inn[1]).astype(bf16)
        vf[1, fL] = (rf[1, fL] + tb[1, 0] * inn[0]).astype(bf16)

    def inner_sweep():
        for b in (0, 1):
            inn[b] = ci[b, F:] + dot(bx[b, F:], vf[b])

    def outer_faces(below, above):
        vf[0, fL] = (rf[0, fL] + tb[0, 0] * below).astype(bf16)
        vf[1, fU] = (rf[1, fU] + tb[1, 1] * above).astype(bf16)

    def ghost(d):
        return dot(mp[d], (rg[d] + tg[d] * gin[d]).astype(bf16))

    count = 2 * ns
    ri = lax.broadcasted_iota(jnp.int32, (count, count), 0)
    ki = lax.broadcasted_iota(jnp.int32, (count, count), 1)
    pieces = -(-(nc - 1) // 3)

    def coarse_piece(w):
        @pl.when(w == 1)
        def _():
            def link(b, a):
                q, g = partner[b], cond[b]
                a = a + jnp.where((ri == b) & (ki == q), g, 0.0)
                return a + jnp.where((ri == q) & (ki == b), g, 0.0)

            chain = jnp.where((ri - ki == 1) | (ki - ri == 1), 1.0, 0.0).astype(f32)
            a = lax.fori_loop(0, count, link, chain)
            gm[...] = jnp.where(ri == ki, 1.0 + jnp.sum(a, axis=1, keepdims=True), 0.0) - a

        @pl.when((w >= 1) & (w <= 4))
        def _():
            def pivot(i, a):
                at = (w - 1) * (count // 4) + i
                col = jnp.sum(jnp.where(ki == at, a, 0.0), axis=1, keepdims=True)
                row = jnp.sum(jnp.where(ri == at, a, 0.0), axis=0, keepdims=True)
                d = jnp.sum(jnp.where(ki[:1] == at, row, 0.0), axis=1, keepdims=True)
                inv_d = 1.0 / d
                scaled = row * inv_d
                new = jnp.where(ri == at, scaled, a - col * scaled)
                new = jnp.where(ki == at, col * inv_d, new)
                return jnp.where((ki == at) & (ri == at), -inv_d, new)

            gm[...] = lax.fori_loop(0, count // 4, pivot, gm[...])

        @pl.when(w == 5)
        def _():
            rw[...] = jnp.zeros_like(rw)

        @pl.when(w >= 5)
        def _():
            rr = lax.broadcasted_iota(jnp.int32, rw.shape, 0)
            unit = lax.bitwise_and(lax.broadcasted_iota(jnp.int32, rw.shape, 1), 7)
            slot = lax.shift_right_logical(lax.broadcasted_iota(jnp.int32, rw.shape, 1), 3)

            def power(i, acc):
                k = (8 - w) * pieces - i
                here = (unit < 2) & (rr - unit == 2 * s) & (slot == c - 1 - k)
                return -jnp.dot(gm[...], acc + jnp.where(here, 1.0, 0.0), precision=HI,
                                preferred_element_type=f32)

            rw[...] = lax.fori_loop(0, pieces, power, rw[...])

        @pl.when(w == 7)
        def _():
            pr = lax.broadcasted_iota(jnp.int32, (8 * ns, count), 0)
            pc = lax.broadcasted_iota(jnp.int32, (8 * ns, count), 1)
            half = lax.bitwise_and(pr, 7)
            spread = jnp.where((half < 2) & (2 * lax.shift_right_logical(pr, 3) + half == pc), 1.0, 0.0)
            rm[...] = jnp.dot(spread.astype(f32), rw[...], precision=HI, preferred_element_type=f32)

    def step(n, _):
        for b in (0, 1):
            vi[b] = (state[b, I] + src[b, I].astype(f32)).astype(bf16)
            rf[b, fL] = state[b, L] + src[b, L].astype(f32)
            rf[b, fU] = state[b, U] + src[b, U].astype(f32)
        inner_faces()
        cn[1, U] = dot(inv[1, U, I], vi[1])
        sbuf[0, Q1] = cn[1, U] + dot(inv[1, U, L], vf[1, fL])
        send(0, Q1)
        cn[0, L] = dot(inv[0, L, I], vi[0])
        sbuf[1, Q1] = cn[0, L] + dot(inv[0, L, U], vf[0, fU])
        send(1, Q1)

        @pl.when(n == 0)
        def _():
            scoarse[...] = jnp.zeros_like(scoarse)
            for b in (0, 1):
                scoarse[pl.ds(b, 1), :] = jnp.sum(state[b], axis=0, keepdims=True) / width
                own_rows(b)
                face[b, :, fL] = inv[b, :, L]
                face[b, :, fU] = inv[b, :, U]

            @pl.when(c > 0)
            def _():
                coarse_back().start()
            arrive(MT)
            for d in (0, 1):
                ghot[d] = chosen(rmt[d, pl.ds(0, 1), :])
                tg[d] = down_rows(rmt[d, pl.ds(1, 1), :])
            for b in (0, 1):
                read = dot(ghot[b], inv[0, L, :] if b == 0 else inv[1, U, :]).astype(bf16)
                bx[b, :F, fL] = read[:, L]
                bx[b, :F, fU] = read[:, U]
                bi[b, :F] = read[:, I]
            gin[0] = pick(ghot[0], state[0, L])
            gin[1] = pick(ghot[1], state[1, U])
            for d in (0, 1):
                @pl.when(recvs[d])
                def _():
                    across(d).wait_recv()
                    for o in range(1, group):
                        along(d, o).start()

        for b in (0, 1):
            ci[b] = dot(bi[b], vi[b])
        cn[0, F:] = dot(inv[0, F:, I], vi[0])
        cn[1, :width - F] = dot(inv[1, :width - F, I], vi[1])
        coarse_piece(2 * n)

        arrive(PF)
        outer_faces(pick(hot[0, 0], rbuf[0, PF]), pick(hot[1, 1], rbuf[1, PF]))
        inner_sweep()

        @pl.when(n == 0)
        def _():
            for d in (0, 1):
                @pl.when(sends[d])
                def _():
                    across(d).wait_send()

                @pl.when(recvs[d])
                def _():
                    for o in range(1, group):
                        along_from(d, o).wait_recv()
                    for o in range(1, group):
                        along(d, o).wait_send()
            mp[0] = dot(hot[0, 0], rst[0, 0].astype(bf16)).astype(bf16)
            mp[1] = dot(hot[1, 1], rst[1, 0].astype(bf16)).astype(bf16)
            sent(MT)

            @pl.when(c == 0)
            def _():
                keep.wait()

        for d in (0, 1):
            rg[d] = rbuf[d, PF] + rst[d, 1]
        more = [ghost(d) for d in (0, 1)]
        arrive(Q1)
        below = pick(hot[0, 0], rbuf[0, Q1]) + more[0]
        above = pick(hot[1, 1], rbuf[1, Q1]) + more[1]
        sent(PF, Q1)

        outer_faces(below, above)
        inner_faces()
        for b in (1, 0):
            y = ci[b] + dot(bx[b], vf[b])
            sbuf[1 - b, U2] = y[:F]
            gin[b] = y[:F]
            inn[b] = y[F:]
            send(1 - b, U2)
        inner_faces()
        sbuf[0, Q3] = ci[1, :F] + dot(bx[1, :F, fL], vf[1, fL])
        send(0, Q3)
        sbuf[1, Q3] = ci[0, :F] + dot(bx[0, :F, fU], vf[0, fU])
        send(1, Q3)
        coarse_piece(2 * n + 1)

        more = [ghost(d) for d in (0, 1)]
        arrive(U2)
        outer_faces(rbuf[0, U2], rbuf[1, U2])
        inner_sweep()
        arrive(Q3)
        below = rbuf[0, Q3] + more[0]
        above = rbuf[1, Q3] + more[1]
        sent(U2, Q3)

        outer_faces(below, above)
        inner_faces()
        state[1, U] = cn[1, U] + dot(face[1, U], vf[1])
        state[0, L] = cn[0, L] + dot(face[0, L], vf[0])

        @pl.when(n < STEPS - 1)
        def _():
            send(0, PF)
            send(1, PF)

        state[1, :width - F] = cn[1, :width - F] + dot(face[1, :width - F], vf[1])
        state[0, F:] = cn[0, F:] + dot(face[0, F:], vf[0])

        @pl.when(n < STEPS - 1)
        def _():
            for b in (0, 1):
                y = ci[b] + dot(bx[b], vf[b])
                gin[b] = y[:F]
                inn[b] = y[F:]
        return 0

    def coarse_back():
        return pltpu.make_async_remote_copy(
            src_ref=scoarse, dst_ref=rcoarse, send_sem=csem, recv_sem=rcsem,
            device_id={"cuts": lax.rem(c + nc - 1, nc)}, device_id_type=MESH)

    lax.fori_loop(0, STEPS, step, 0)

    def end(b):
        return pltpu.make_async_remote_copy(
            src_ref=state.at[b], dst_ref=prev.at[b], send_sem=esem.at[b], recv_sem=resem.at[b],
            device_id={"cuts": lax.rem(c + 1, nc)}, device_id_type=MESH)

    def jump(o):
        return pltpu.make_async_remote_copy(
            src_ref=hb, dst_ref=hs.at[c], send_sem=hsem.at[o], recv_sem=rhsem.at[c],
            device_id={"cuts": lax.rem(c + o, nc)}, device_id_type=MESH)

    def jump_from(o):
        at = lax.rem(c + nc - o, nc)
        return pltpu.make_async_remote_copy(
            src_ref=hb, dst_ref=hs.at[at], send_sem=hsem.at[o], recv_sem=rhsem.at[at],
            device_id={"cuts": at}, device_id_type=MESH)

    def part(o):
        to = lax.rem(s + o, ns)
        return pltpu.make_async_remote_copy(
            src_ref=zb.at[to], dst_ref=zs.at[s], send_sem=zsem.at[o], recv_sem=rzsem.at[s],
            device_id={"sub": to}, device_id_type=MESH)

    def part_from(o):
        at = lax.rem(s + ns - o, ns)
        return pltpu.make_async_remote_copy(
            src_ref=zb.at[at], dst_ref=zs.at[at], send_sem=zsem.at[o], recv_sem=rzsem.at[at],
            device_id={"sub": at}, device_id_type=MESH)

    @pl.when(c < nc - 1)
    def _():
        coarse_back().wait_recv()

    for b in (0, 1):
        hb[pl.ds(b, 1), :] = jnp.sum(state[b], axis=0, keepdims=True) / width - rcoarse[pl.ds(b, 1), :]
    for o in range(2, nc):
        @pl.when(c + o < nc)
        def _():
            jump(o).start()

    @pl.when(c < nc - 1)
    def _():
        for b in (0, 1):
            end(b).start()

    @pl.when(c > 0)
    def _():
        coarse_back().wait_send()

    for o in range(2, nc):
        @pl.when(c - o >= 0)
        def _():
            jump_from(o).wait_recv()

    z = jnp.dot(rm[...], hs[...].reshape(8 * nc, F), precision=HI, preferred_element_type=f32)
    zb[...] = z.reshape(ns, 8, F)
    for o in range(1, ns):
        part(o).start()
    for o in range(1, ns):
        part_from(o).wait_recv()
    zs[s] = zb[s]
    wout[...] = jnp.sum(zs[...], axis=0)[:2]

    @pl.when(c > 0)
    def _():
        for b in (0, 1):
            end(b).wait_recv()

    for o in range(2, nc):
        @pl.when(c + o < nc)
        def _():
            jump(o).wait_send()
    for o in range(1, ns):
        part(o).wait_send()

    @pl.when(c < nc - 1)
    def _():
        for b in (0, 1):
            end(b).wait_send()


def solution(mesh):
    ns, nc = mesh.shape["sub"], mesh.shape["cuts"]

    def on_device(start, source, inverse, face_map, trans, partner, cond):
        width, cols = start.shape[2:]
        any_ = pl.BlockSpec(memory_space=pl.ANY)
        vmem = pl.BlockSpec(memory_space=pltpu.VMEM)
        smem = pl.BlockSpec(memory_space=pltpu.SMEM)
        V, S = pltpu.VMEM, pltpu.SemaphoreType.DMA
        scratch = dict(
            state=V((2, width, cols), f32), src=V((2, width, cols), bf16), inv=V((2, width, width), bf16),
            face=V((2, width, 2 * F), bf16), rf=V((2, 2 * F, cols), f32), vf=V((2, 2 * F, cols), bf16),
            vi=V((2, width - 2 * F, cols), bf16), cn=V((2, width, cols), f32), ci=V((2, 2 * F, cols), f32),
            bx=V((2, 2 * F, 2 * F), bf16), bi=V((2, 2 * F, width - 2 * F), bf16),
            sbuf=V((2, 4, F, cols), f32), rbuf=V((2, 4, F, cols), f32),
            smt=V((2, 8, F), f32), rmt=V((2, 8, F), f32), sst=V((2, 2, F, cols), f32), rst=V((2, 2, F, cols), f32),
            inn=V((2, F, cols), f32), gin=V((2, F, cols), f32), rg=V((2, F, cols), f32),
            tb=V((2, 2, F, cols), f32), tg=V((2, F, cols), f32),
            hot=V((2, 2, F, F), bf16), ghot=V((2, F, F), bf16), mp=V((2, F, F), bf16),
            scoarse=V((8, cols), f32), rcoarse=V((8, cols), f32),
            hs=V((nc, 8, cols), f32), zb=V((ns, 8, cols), f32), zs=V((ns, 8, cols), f32),
            hb=V((8, cols), f32), gm=V((2 * ns, 2 * ns), f32), rm=V((8 * ns, 8 * nc), f32),
            rw=V((2 * ns, 8 * nc), f32),
            lsem=S((4,)), ssem=S((2, 5)), rsem=S((2, 5)), psem=S((2,)), rpsem=S((2,)),
            fsem=S((2, 8)), rfsem=S((2, 8)), esem=S((2,)), resem=S((2,)),
            csem=S(()), rcsem=S(()), hsem=S((nc,)), rhsem=S((nc,)), zsem=S((ns,)), rzsem=S((ns,)),
        )
        ends, added = pl.pallas_call(
            functools.partial(kernel, ns, nc),
            out_shape=(jax.ShapeDtypeStruct(start.shape[1:], f32), jax.ShapeDtypeStruct((2, cols), f32)),
            in_specs=[smem, smem, any_, any_, any_, vmem, vmem],
            out_specs=(any_, vmem),
            scratch_shapes=list(scratch.values()),
            compiler_params=pltpu.CompilerParams(collective_id=0, has_side_effects=True),
            name="parareal",
        )(partner, cond, start, source, inverse, face_map, trans)
        return (ends + added[:, None, :])[None]

    in_specs = (
        P("cuts", "sub", None, None),
        P("sub", None, None),
        P("sub", None, None),
        P("sub", None, None),
        P("sub", None, None),
        P(),
        P(),
    )
    return jax.shard_map(on_device, mesh=mesh, in_specs=in_specs,
                         out_specs=P("cuts", "sub", None, None), check_vma=False)
```

time: 97.9 us -> 93.3 us (0.953)
  Pallas kernels: 95 us -> 90.6 us
  other arithmetic: 0 us -> 1.87 us
  local copies, waits for them, and re-layouts: 1.87 us -> 0.66 us
    pallas_call x1, Pallas kernels: 95 us -> 90.6 us  [on_device(): pl.pallas_call(functools.partial(kernel, ns, nc), out_shape=(jax.ShapeDty...]
    broadcast_in_dim x0 -> x1, other arithmetic: none -> 1.87 us  [on_device(): return (ends + added[:, None, :])[None]]
    unnamed x1 -> x2, local copies, waits for them, and re-layouts: 1.87 us -> 0.66 us
where the time goes in v1:
time: 93.3 us; the launch traced here: 93.1 us
  Pallas kernels  90.6 us (97%)
  other arithmetic  1.87 us (2%)
    pallas_call x1, Pallas kernels, on_device(): pl.pallas_call(functools.partial(kernel, ns, nc), out_shape=(jax.ShapeDty...  90.6 us
    broadcast_in_dim x1, other arithmetic, on_device(): return (ends + added[:, None, :])[None]  1.87 us

profile of v1, /device:TPU:32, one launch (start us, length us, event | category | flops | bytes accessed | tf_op | source)
XLA Modules:
  0.0 93.1 jit_solution(11610711900355354874)
XLA Ops:
  0.0 90.6 %parareal.1 = (f32[2,512,128]{2,1,0:T(8,128)}, f32[2,128]{1,0:T(2,128)}) custom-call(s32[32]{0:T(128)} %partner.1, f32[32]{0:T(128)} %cond.1, f32[1,2,512,128]{3,2,1,0:T(8,128)} %start_h.1, bf16[2,512,128]{2,1,0:T(8,128)(2,1)} %source_h.1, bf16[2,512,512]{2,1,0:T(8,128)(2,1)} %inv_h.1, s32[2,2,128]{2,1,0:T(2,128)} %fmap.1, f32[2,2,128]{2,1,0:T(2,128)} %trans.1), custom_call_target="tpu_custom_call" | custom-call | tf_op jit(solution)/shard_map/parareal/pallas_call | solution.py:494
  90.6 0.0 copy-start
  90.6 0.7 copy-done
  91.3 1.9 %add_bitcast_fusion = f32[1,2,512,128]{3,2,1,0:T(8,128)} fusion(f32[2,512,128]{2,1,0:T(8,128)} %get-tuple-element.7, f32[2,128]{1,0:T(2,128)S(1)} %copy-done), kind=kLoop, calls=%fused_computation | loop fusion | flops 131072 | bytes 1049600 | tf_op jit(solution)/shard_map/broadcast_in_dim | solution.py:503
Async XLA Ops:
  90.6 0.7 copy-start

commit v2 on v1

--- a/solution.py
+++ b/solution.py
@@ -36,7 +36,8 @@
     return both[:, :F] + both[:, F:]
 
 
-def kernel(ns, nc, partner, cond, start_h, source_h, inv_h, fmap, trans, prev, wout,
+def kernel(ns, nc, partner_h, cond_h, start_h, source_h, inv_h, fmap_h, trans_h, prev,
+           partner, cond, fmap, trans,
            state, src, inv, face, rf, vf, vi, cn, ci, bx, bi, sbuf, rbuf, smt, rmt, sst, rst,
            inn, gin, rg, tb, tg, hot, ghot, mp, scoarse, rcoarse, hs, zb, zs, hb, gm, rm, rw,
            lsem, ssem, rsem, psem, rpsem, fsem, rfsem, esem, resem, csem, rcsem, hsem, rhsem, zsem, rzsem):
@@ -50,9 +51,13 @@
         pltpu.make_async_copy(start_h.at[0], state, lsem.at[0]),
         pltpu.make_async_copy(source_h, src, lsem.at[1]),
         pltpu.make_async_copy(inv_h, inv, lsem.at[2]),
+        pltpu.make_async_copy(fmap_h, fmap, lsem.at[4]),
+        pltpu.make_async_copy(trans_h, trans, lsem.at[5]),
+        pltpu.make_async_copy(partner_h, partner, lsem.at[6]),
+        pltpu.make_async_copy(cond_h, cond, lsem.at[7]),
     ]
-    for load in loads:
-        load.start()
+    for k in (3, 4, 0, 1, 2, 5, 6):
+        loads[k].start()
 
     hs[...] = jnp.zeros_like(hs)
     hb[...] = jnp.zeros_like(hb)
@@ -132,6 +137,8 @@
             rmt[d] = jnp.zeros(rmt.shape[1:], f32)
             rst[d] = jnp.zeros(rst.shape[1:], f32)
 
+    loads[3].wait()
+    loads[4].wait()
     rows = [[fmap[b, pl.ds(k, 1), :].astype(f32) for k in (0, 1)] for b in (0, 1)]
     trow = [[trans[b, pl.ds(k, 1), :] for k in (0, 1)] for b in (0, 1)]
     smt[...] = jnp.zeros_like(smt)
@@ -145,7 +152,7 @@
             hot[b, k] = chosen(rows[b][k])
 
     loads[0].wait()
-    keep = pltpu.make_async_copy(state, prev, lsem.at[3])
+    keep = pltpu.make_async_copy(start_h.at[0], prev.at[0], lsem.at[3])
 
     @pl.when(c == 0)
     def _():
@@ -161,11 +168,11 @@
     pl.semaphore_wait(barrier, ns - 1 + nc - 1)
 
     for d in (0, 1):
+        @pl.when(sends[d])
+        def _():
+            across(d).start()
+
         send(d, MT, PF)
-
-        @pl.when(sends[d])
-        def _():
-            across(d).start()
 
     def own_rows(b):
         rows_of = dot(hot[1, 0], inv[0, U, :]) if b == 0 else dot(hot[0, 1], inv[1, L, :])
@@ -320,9 +327,8 @@
             mp[1] = dot(hot[1, 1], rst[1, 0].astype(bf16)).astype(bf16)
             sent(MT)
 
-            @pl.when(c == 0)
-            def _():
-                keep.wait()
+            loads[5].wait()
+            loads[6].wait()
 
         for d in (0, 1):
             rg[d] = rbuf[d, PF] + rst[d, 1]
@@ -386,7 +392,7 @@
 
     def end(b):
         return pltpu.make_async_remote_copy(
-            src_ref=state.at[b], dst_ref=prev.at[b], send_sem=esem.at[b], recv_sem=resem.at[b],
+            src_ref=state.at[b], dst_ref=prev.at[0, b], send_sem=esem.at[b], recv_sem=resem.at[b],
             device_id={"cuts": lax.rem(c + 1, nc)}, device_id_type=MESH)
 
     def jump(o):
@@ -444,12 +450,17 @@
     for o in range(1, ns):
         part_from(o).wait_recv()
     zs[s] = zb[s]
-    wout[...] = jnp.sum(zs[...], axis=0)[:2]
+    added = jnp.sum(zs[...], axis=0)
+
+    @pl.when(c == 0)
+    def _():
+        keep.wait()
 
     @pl.when(c > 0)
     def _():
         for b in (0, 1):
             end(b).wait_recv()
+            prev[0, b] = prev[0, b] + jnp.broadcast_to(added[b:b + 1], (width, F))
 
     for o in range(2, nc):
         @pl.when(c + o < nc)
@@ -471,9 +482,10 @@
         width, cols = start.shape[2:]
         any_ = pl.BlockSpec(memory_space=pl.ANY)
         vmem = pl.BlockSpec(memory_space=pltpu.VMEM)
-        smem = pl.BlockSpec(memory_space=pltpu.SMEM)
         V, S = pltpu.VMEM, pltpu.SemaphoreType.DMA
         scratch = dict(
+            partner=pltpu.SMEM(partner.shape, jnp.int32), cond=pltpu.SMEM(cond.shape, f32),
+            fmap=V(face_map.shape, jnp.int32), trans=V(trans.shape, f32),
             state=V((2, width, cols), f32), src=V((2, width, cols), bf16), inv=V((2, width, width), bf16),
             face=V((2, width, 2 * F), bf16), rf=V((2, 2 * F, cols), f32), vf=V((2, 2 * F, cols), bf16),
             vi=V((2, width - 2 * F, cols), bf16), cn=V((2, width, cols), f32), ci=V((2, 2 * F, cols), f32),
@@ -487,20 +499,21 @@
             hs=V((nc, 8, cols), f32), zb=V((ns, 8, cols), f32), zs=V((ns, 8, cols), f32),
             hb=V((8, cols), f32), gm=V((2 * ns, 2 * ns), f32), rm=V((8 * ns, 8 * nc), f32),
             rw=V((2 * ns, 8 * nc), f32),
-            lsem=S((4,)), ssem=S((2, 5)), rsem=S((2, 5)), psem=S((2,)), rpsem=S((2,)),
+            lsem=S((8,)), ssem=S((2, 5)), rsem=S((2, 5)), psem=S((2,)), rpsem=S((2,)),
             fsem=S((2, 8)), rfsem=S((2, 8)), esem=S((2,)), resem=S((2,)),
             csem=S(()), rcsem=S(()), hsem=S((nc,)), rhsem=S((nc,)), zsem=S((ns,)), rzsem=S((ns,)),
         )
-        ends, added = pl.pallas_call(
+        return pl.pallas_call(
             functools.partial(kernel, ns, nc),
-            out_shape=(jax.ShapeDtypeStruct(start.shape[1:], f32), jax.ShapeDtypeStruct((2, cols), f32)),
-            in_specs=[smem, smem, any_, any_, any_, vmem, vmem],
-            out_specs=(any_, vmem),
+            out_shape=pltpu.VMEM(start.shape, f32),
+            in_specs=[any_] * 7,
+            out_specs=vmem,
             scratch_shapes=list(scratch.values()),
-            compiler_params=pltpu.CompilerParams(collective_id=0, has_side_effects=True),
+            compiler_params=pltpu.CompilerParams(collective_id=0, has_side_effects=True,
+                                                 vmem_limit_bytes=40 * 2**20),
             name="parareal",
-        )(partner, cond, start, source, inverse, face_map, trans)
-        return (ends + added[:, None, :])[None]
+        )(*[pltpu.with_memory_space_constraint(a, pltpu.HBM)
+            for a in (partner, cond, start, source, inverse, face_map, trans)])
 
     in_specs = (
         P("cuts", "sub", None, None),

time: 93.3 us -> 88.9 us (0.953)
  Pallas kernels: 90.6 us -> 88 us
  other arithmetic: 1.87 us -> 0 us
    pallas_call x1, Pallas kernels: 90.6 us -> 88 us  [on_device(): pl.pallas_call(functools.partial(kernel, ns, nc), out_shape=pltpu.VMEM(st...]
    broadcast_in_dim x1 -> x0, other arithmetic: 1.87 us -> none  [on_device(): return (ends + added[:, None, :])[None]]
where the time goes in v2:
time: 88.9 us; the launch traced here: 88.8 us
  Pallas kernels  88 us (99%)
    pallas_call x1, Pallas kernels, on_device(): pl.pallas_call(functools.partial(kernel, ns, nc), out_shape=pltpu.VMEM(st...  88 us

profile of v2, /device:TPU:32, one launch (start us, length us, event | category | flops | bytes accessed | tf_op | source)
XLA Modules:
  0.0 88.8 jit_solution(4406714869010773556)
XLA Ops:
  0.0 88.0 %parareal.1 = f32[1,2,512,128]{3,2,1,0:T(8,128)S(1)} custom-call(s32[32]{0:T(128)} %partner_h.1, f32[32]{0:T(128)} %cond_h.1, f32[1,2,512,128]{3,2,1,0:T(8,128)} %start_h.1, bf16[2,512,128]{2,1,0:T(8,128)(2,1)} %source_h.1, bf16[2,512,512]{2,1,0:T(8,128)(2,1)} %inv_h.1, s32[2,2,128]{2,1,0:T(2,128)} %fmap_h.1, f32[2,2,128]{2,1,0:T(2,128)} %trans_h.1), custom_call_target="tpu_custom_call" | custom-call | tf_op jit(solution)/shard_map/parareal/pallas_call | solution.py:506
  88.0 0.8 copy.9

commit v3 on v2

--- a/solution.py
+++ b/solution.py
@@ -9,10 +9,13 @@
 
 F = 128
 STEPS = 4
+PARTS = 4
+ROW = 4
 MESH = pl.DeviceIdType.MESH
 f32, bf16 = jnp.float32, jnp.bfloat16
 HI = lax.Precision.HIGHEST
 PF, Q1, U2, Q3, MT = range(5)
+VIA = (Q1, Q3,)
 
 
 def dot(a, b):
@@ -40,7 +43,7 @@
            partner, cond, fmap, trans,
            state, src, inv, face, rf, vf, vi, cn, ci, bx, bi, sbuf, rbuf, smt, rmt, sst, rst,
            inn, gin, rg, tb, tg, hot, ghot, mp, scoarse, rcoarse, hs, zb, zs, hb, gm, rm, rw,
-           lsem, ssem, rsem, psem, rpsem, fsem, rfsem, esem, resem, csem, rcsem, hsem, rhsem, zsem, rzsem):
+           held, heldsem, passsem, freesem, lsem, ssem, rsem, psem, rpsem, fsem, rfsem, esem, resem, csem, rcsem, hsem, rhsem, zsem, rzsem):
     c, s = lax.axis_index("cuts"), lax.axis_index("sub")
     width = state.shape[1]
     L, U, I = slice(0, F), slice(width - F, width), slice(F, width - F)
@@ -72,26 +75,87 @@
     def towards(d):
         return lax.rem(s + 1, ns) if d == 0 else lax.rem(s + ns - 1, ns)
 
+    def ext_source(d, i):
+        if i == MT:
+            return smt.at[d]
+        if i == PF:
+            return state.at[1, pl.ds(width - F, F)] if d == 0 else state.at[0, pl.ds(0, F)]
+        return sbuf.at[d, i]
+
     def ext(d, i):
-        if i == MT:
-            a, b = smt.at[d], rmt.at[d]
-        elif i == PF:
-            a = state.at[1, pl.ds(width - F, F)] if d == 0 else state.at[0, pl.ds(0, F)]
-            b = rbuf.at[d, i]
-        else:
-            a, b = sbuf.at[d, i], rbuf.at[d, i]
-        return pltpu.make_async_remote_copy(
-            src_ref=a, dst_ref=b, send_sem=ssem.at[d, i], recv_sem=rsem.at[d, i],
+        return pltpu.make_async_remote_copy(
+            src_ref=ext_source(d, i), dst_ref=rmt.at[d] if i == MT else rbuf.at[d, i], send_sem=ssem.at[d, i], recv_sem=rsem.at[d, i],
             device_id={"sub": towards(d)}, device_id_type=MESH)
 
     sends = (has_above, has_below)
     recvs = (has_below, has_above)
 
+    odd = lax.rem(c, 2) == 1
+    at = lax.rem(s, ROW)
+    leaves = (odd & (at == ROW - 1) & has_above, odd & (at == 0) & has_below)
+    serves = (odd & (at == 0) & (s + ROW < ns), odd & (at == ROW - 1) & (s >= ROW))
+
+    def part_of(ref, h):
+        return ref.at[pl.ds(h * (F // PARTS), F // PARTS)]
+
+    def first_leg(d, i, h):
+        step = ns + 1 - ROW if d == 0 else ROW - 1
+        return pltpu.make_async_remote_copy(
+            src_ref=part_of(ext_source(d, i), h), dst_ref=part_of(held.at[d, i], h),
+            send_sem=ssem.at[d, i], recv_sem=heldsem.at[d, i, h],
+            device_id={"sub": lax.rem(s + step, ns)}, device_id_type=MESH)
+
+    def second_leg(d, i, h=None):
+        step = ROW if d == 0 else ns - ROW
+        return pltpu.make_async_remote_copy(
+            src_ref=held.at[d, i] if h is None else part_of(held.at[d, i], h),
+            dst_ref=rbuf.at[d, i] if h is None else part_of(rbuf.at[d, i], h), send_sem=passsem.at[d, i], recv_sem=rsem.at[d, i],
+            device_id={"sub": lax.rem(s + step, ns)}, device_id_type=MESH)
+
+    def pass_on(*which):
+        for d in (0, 1):
+            @pl.when(serves[d])
+            def _():
+                for i in which:
+                    for h in range(PARTS):
+                        first_leg(d, i, h).wait_recv()
+                        second_leg(d, i, h).start()
+
+    def granted(n, i):
+        for d in (0, 1):
+            @pl.when(leaves[d] & (n > 0))
+            def _():
+                pl.semaphore_wait(freesem.at[d, i], 1)
+
+    def grant(n, i):
+        for d in (0, 1):
+            source = lax.rem(s + (ROW - 1 if d == 0 else ns + 1 - ROW), ns)
+
+            @pl.when(serves[d] & (n < STEPS - 1))
+            def _():
+                pl.semaphore_signal(freesem.at[d, i], inc=1, device_id={"sub": source}, device_id_type=MESH)
+
+    def passed_on(*which):
+        for d in (0, 1):
+            @pl.when(serves[d])
+            def _():
+                for i in which:
+                    second_leg(d, i).wait_send()
+
     def send(d, *which):
-        @pl.when(sends[d])
+        @pl.when(sends[d] & jnp.logical_not(leaves[d]))
         def _():
             for i in which:
                 ext(d, i).start()
+
+        @pl.when(leaves[d])
+        def _():
+            for i in which:
+                if i in VIA:
+                    for h in range(PARTS):
+                        first_leg(d, i, h).start()
+                else:
+                    ext(d, i).start()
 
     def sent(*which):
         for d in (0, 1):
@@ -263,6 +327,7 @@
             rf[b, fL] = state[b, L] + src[b, L].astype(f32)
             rf[b, fU] = state[b, U] + src[b, U].astype(f32)
         inner_faces()
+        granted(n, Q1)
         cn[1, U] = dot(inv[1, U, I], vi[1])
         sbuf[0, Q1] = cn[1, U] + dot(inv[1, U, L], vf[1, fL])
         send(0, Q1)
@@ -282,6 +347,7 @@
             @pl.when(c > 0)
             def _():
                 coarse_back().start()
+            pass_on(Q1)
             arrive(MT)
             for d in (0, 1):
                 ghot[d] = chosen(rmt[d, pl.ds(0, 1), :])
@@ -306,6 +372,10 @@
         cn[1, :width - F] = dot(inv[1, :width - F, I], vi[1])
         coarse_piece(2 * n)
 
+        @pl.when(n > 0)
+        def _():
+            pass_on(Q1)
+
         arrive(PF)
         outer_faces(pick(hot[0, 0], rbuf[0, PF]), pick(hot[1, 1], rbuf[1, PF]))
         inner_sweep()
@@ -337,6 +407,8 @@
         below = pick(hot[0, 0], rbuf[0, Q1]) + more[0]
         above = pick(hot[1, 1], rbuf[1, Q1]) + more[1]
         sent(PF, Q1)
+        passed_on(Q1)
+        grant(n, Q1)
 
         outer_faces(below, above)
         inner_faces()
@@ -347,6 +419,7 @@
             inn[b] = y[F:]
             send(1 - b, U2)
         inner_faces()
+        granted(n, Q3)
         sbuf[0, Q3] = ci[1, :F] + dot(bx[1, :F, fL], vf[1, fL])
         send(0, Q3)
         sbuf[1, Q3] = ci[0, :F] + dot(bx[0, :F, fU], vf[0, fU])
@@ -354,6 +427,7 @@
         coarse_piece(2 * n + 1)
 
         more = [ghost(d) for d in (0, 1)]
+        pass_on(Q3)
         arrive(U2)
         outer_faces(rbuf[0, U2], rbuf[1, U2])
         inner_sweep()
@@ -361,6 +435,8 @@
         below = rbuf[0, Q3] + more[0]
         above = rbuf[1, Q3] + more[1]
         sent(U2, Q3)
+        passed_on(Q3)
+        grant(n, Q3)
 
         outer_faces(below, above)
         inner_faces()
@@ -499,7 +575,7 @@
             hs=V((nc, 8, cols), f32), zb=V((ns, 8, cols), f32), zs=V((ns, 8, cols), f32),
             hb=V((8, cols), f32), gm=V((2 * ns, 2 * ns), f32), rm=V((8 * ns, 8 * nc), f32),
             rw=V((2 * ns, 8 * nc), f32),
-            lsem=S((8,)), ssem=S((2, 5)), rsem=S((2, 5)), psem=S((2,)), rpsem=S((2,)),
+            held=V((2, 4, F, cols), f32), heldsem=S((2, 4, PARTS)), passsem=S((2, 4)), freesem=pltpu.SemaphoreType.REGULAR((2, 4)), lsem=S((8,)), ssem=S((2, 5)), rsem=S((2, 5)), psem=S((2,)), rpsem=S((2,)),
             fsem=S((2, 8)), rfsem=S((2, 8)), esem=S((2,)), resem=S((2,)),
             csem=S(()), rcsem=S(()), hsem=S((nc,)), rhsem=S((nc,)), zsem=S((ns,)), rzsem=S((ns,)),
         )

time: 88.9 us -> 87.8 us (0.988)
  Pallas kernels: 88 us -> 86.9 us
    pallas_call x1, Pallas kernels: 88 us -> 86.9 us  [on_device(): pl.pallas_call(functools.partial(kernel, ns, nc), out_shape=pltpu.VMEM(st...]
where the time goes in v3:
time: 87.8 us; the launch traced here: 87.7 us
  Pallas kernels  86.9 us (99%)
    pallas_call x1, Pallas kernels, on_device(): pl.pallas_call(functools.partial(kernel, ns, nc), out_shape=pltpu.VMEM(st...  86.9 us

profile of v3, /device:TPU:32, one launch (start us, length us, event | category | flops | bytes accessed | tf_op | source)
XLA Modules:
  0.0 87.7 jit_solution(942127981525320854)
XLA Ops:
  0.0 86.9 %parareal.1 = f32[1,2,512,128]{3,2,1,0:T(8,128)S(1)} custom-call(s32[32]{0:T(128)} %partner_h.1, f32[32]{0:T(128)} %cond_h.1, f32[1,2,512,128]{3,2,1,0:T(8,128)} %start_h.1, bf16[2,512,128]{2,1,0:T(8,128)(2,1)} %source_h.1, bf16[2,512,512]{2,1,0:T(8,128)(2,1)} %inv_h.1, s32[2,2,128]{2,1,0:T(2,128)} %fmap_h.1, f32[2,2,128]{2,1,0:T(2,128)} %trans_h.1), custom_call_target="tpu_custom_call" | custom-call | tf_op jit(solution)/shard_map/parareal/pallas_call | solution.py:582
  86.9 0.8 copy.9

commit v4 on v3

--- a/solution.py
+++ b/solution.py
@@ -9,7 +9,7 @@
 
 F = 128
 STEPS = 4
-PARTS = 4
+PARTS = 8
 ROW = 4
 MESH = pl.DeviceIdType.MESH
 f32, bf16 = jnp.float32, jnp.bfloat16
@@ -347,6 +347,12 @@
             @pl.when(c > 0)
             def _():
                 coarse_back().start()
+            for d in (0, 1):
+                @pl.when(recvs[d])
+                def _():
+                    across(d).wait_recv()
+                    for o in range(1, group):
+                        along(d, o).start()
             pass_on(Q1)
             arrive(MT)
             for d in (0, 1):
@@ -359,12 +365,6 @@
                 bi[b, :F] = read[:, I]
             gin[0] = pick(ghot[0], state[0, L])
             gin[1] = pick(ghot[1], state[1, U])
-            for d in (0, 1):
-                @pl.when(recvs[d])
-                def _():
-                    across(d).wait_recv()
-                    for o in range(1, group):
-                        along(d, o).start()
 
         for b in (0, 1):
             ci[b] = dot(bi[b], vi[b])
@@ -417,13 +417,12 @@
             sbuf[1 - b, U2] = y[:F]
             gin[b] = y[:F]
             inn[b] = y[F:]
-            send(1 - b, U2)
         inner_faces()
         granted(n, Q3)
         sbuf[0, Q3] = ci[1, :F] + dot(bx[1, :F, fL], vf[1, fL])
-        send(0, Q3)
         sbuf[1, Q3] = ci[0, :F] + dot(bx[0, :F, fU], vf[0, fU])
-        send(1, Q3)
+        for d in (0, 1):
+            send(d, U2, Q3)
         coarse_piece(2 * n + 1)
 
         more = [ghost(d) for d in (0, 1)]

time: 87.8 us -> 85.8 us (0.977)
  Pallas kernels: 86.9 us -> 84.9 us
    pallas_call x1, Pallas kernels: 86.9 us -> 84.9 us  [on_device(): pl.pallas_call(functools.partial(kernel, ns, nc), out_shape=pltpu.VMEM(st...]
where the time goes in v4:
time: 85.8 us; the launch traced here: 85.7 us
  Pallas kernels  84.9 us (99%)
    pallas_call x1, Pallas kernels, on_device(): pl.pallas_call(functools.partial(kernel, ns, nc), out_shape=pltpu.VMEM(st...  84.9 us

profile of v4, /device:TPU:32, one launch (start us, length us, event | category | flops | bytes accessed | tf_op | source)
XLA Modules:
  0.0 85.7 jit_solution(5037407226031897024)
XLA Ops:
  0.0 84.9 %parareal.1 = f32[1,2,512,128]{3,2,1,0:T(8,128)S(1)} custom-call(s32[32]{0:T(128)} %partner_h.1, f32[32]{0:T(128)} %cond_h.1, f32[1,2,512,128]{3,2,1,0:T(8,128)} %start_h.1, bf16[2,512,128]{2,1,0:T(8,128)(2,1)} %source_h.1, bf16[2,512,512]{2,1,0:T(8,128)(2,1)} %inv_h.1, s32[2,2,128]{2,1,0:T(2,128)} %fmap_h.1, f32[2,2,128]{2,1,0:T(2,128)} %trans_h.1), custom_call_target="tpu_custom_call" | custom-call | tf_op jit(solution)/shard_map/parareal/pallas_call | solution.py:581
  84.9 0.8 copy.9

commit v5 on v4

--- a/solution.py
+++ b/solution.py
@@ -499,7 +499,7 @@
 
     for b in (0, 1):
         hb[pl.ds(b, 1), :] = jnp.sum(state[b], axis=0, keepdims=True) / width - rcoarse[pl.ds(b, 1), :]
-    for o in range(2, nc):
+    for o in reversed(range(2, nc)):
         @pl.when(c + o < nc)
         def _():
             jump(o).start()
@@ -520,7 +520,7 @@
 
     z = jnp.dot(rm[...], hs[...].reshape(8 * nc, F), precision=HI, preferred_element_type=f32)
     zb[...] = z.reshape(ns, 8, F)
-    for o in range(1, ns):
+    for o in sorted(range(1, ns), key=lambda o: -min(o, ns - o)):
         part(o).start()
     for o in range(1, ns):
         part_from(o).wait_recv()

time: 85.8 us -> 86.1 us (level)
  no operation moved by 1% of the time
where the time goes in v5:
time: 86.1 us; the launch traced here: 86 us
  Pallas kernels  85.2 us (99%)
    pallas_call x1, Pallas kernels, on_device(): pl.pallas_call(functools.partial(kernel, ns, nc), out_shape=pltpu.VMEM(st...  85.2 us

profile of v5, /device:TPU:32, one launch (start us, length us, event | category | flops | bytes accessed | tf_op | source)
XLA Modules:
  0.0 86.0 jit_solution(1033735670675525812)
XLA Ops:
  0.0 85.2 %parareal.1 = f32[1,2,512,128]{3,2,1,0:T(8,128)S(1)} custom-call(s32[32]{0:T(128)} %partner_h.1, f32[32]{0:T(128)} %cond_h.1, f32[1,2,512,128]{3,2,1,0:T(8,128)} %start_h.1, bf16[2,512,128]{2,1,0:T(8,128)(2,1)} %source_h.1, bf16[2,512,512]{2,1,0:T(8,128)(2,1)} %inv_h.1, s32[2,2,128]{2,1,0:T(2,128)} %fmap_h.1, f32[2,2,128]{2,1,0:T(2,128)} %trans_h.1), custom_call_target="tpu_custom_call" | custom-call | tf_op jit(solution)/shard_map/parareal/pallas_call | solution.py:581
  85.2 0.8 copy.9
